TPU v7x, 32 devices: a whole 2x2x4 slice. The times are simulated.
32 devices in a mesh: groups: 2 (over y), seq: 8 (over z, x), tp: 2 (over core).
Axes of the slice: x: 2, y: 2, z: 4, core: 2. Of those that a mesh axis runs over, the one named last changes fastest.
Arguments:
- stream: bfloat16 [128, 6144], P(('groups', 'seq'), 'tp'), parts along dimension 0, may hold values from -6 to 6
- queries: bfloat16 [128, 6144], P(('groups', 'seq'), 'tp'), parts along dimension 0, may hold values from -6 to 6
- key_rows: bfloat16 [128, 1024], P(('groups', 'seq'), 'tp'), parts along dimension 0, may hold values from -6 to 6
- value_rows: bfloat16 [128, 1024], P(('groups', 'seq'), 'tp'), parts along dimension 0, may hold values from -6 to 6
- routes: int32 [128, 2], P(('groups', 'seq')), parts along dimension 0, may hold values from 0 to 3, all different within a row; in each aligned block of 8 rows (0 to 7, 8 to 15, ...) at most 4 rows name the same one
- seq_length: int32 [2], P('groups'), parts along dimension 0, may hold values from 16 to 64
- norm_gain: float32 [6144], P('tp'), may hold values from 0.25 to 1.75
- router: float32 [6144, 4], P('tp'), may hold values from -0.078125 to 0.078125
- w_up: bfloat16 [6144, 32768], P('tp', 'seq'), may hold values from -0.078125 to 0.078125
- w_down: bfloat16 [32768, 6144], P('seq', 'tp'), may hold values from -0.0625 to 0.0625
- final_gain: float32 [6144], P('tp'), may hold values from 0.25 to 1.75
- value_weight: float32 [6144], P('tp'), may hold values from -0.078125 to 0.078125
- value_bias: float32 [1], replicated, may hold values from -3 to 3
Outputs:
- layer_out: bfloat16 [128, 6144], P(('groups', 'seq'), 'tp'), parts along dimension 0
- values: float32 [128], P(('groups', 'seq')), parts along dimension 0
There are 2 independent parts, one for each index of `groups`. A program takes and returns all parts, laid end to end along the dimension named above; an argument that names none is the same for every part. Nothing has to cross between parts.
Inputs may be any that keep to these rules, and one draw needn't show every extreme that they name: `routes`: each row names two different experts; among the rows on one device no expert is named more than 4 times, and some device's rows name some expert exactly 4 times.
All inputs are finite; a program needn't handle non-finite values.
Results may differ from a plain program's by a relative error of at most 0.01.
Values may be sent and summed in bfloat16 or wider, within the bound.
A program may use at most 128 MiB of HBM per device.

v0:
```python
import functools
import math

import jax
import jax.numpy as jnp
from jax import lax
from jax.experimental import pallas as pl
from jax.experimental.pallas import tpu as pltpu
from jax.sharding import PartitionSpec as P

HD = 128
LANES = 128
SUB = 8
ROW_LIMIT = 64
VMEM_BYTES = 66 * 1000 * 1000

eps = 1e-05
masked = -1e30
MESH = pl.DeviceIdType.MESH


def remote(src, dst, send_sem, recv_sem, device):
    return pltpu.make_async_remote_copy(
        src_ref=src,
        dst_ref=dst,
        send_sem=send_sem,
        recv_sem=recv_sem,
        device_id=device,
        device_id_type=MESH,
    )


def largest(size, most):
    return max(w for w in range(LANES, most + 1, LANES) if size % w == 0)


def block_of(index, size, count):
    block = jnp.zeros_like(index)
    for step in range(1, count):
        block = block + (index >= step * size).astype(jnp.int32)
    return block


def layer_kernel(
    n,
    experts,
    width,
    *refs,
):
    inputs, (out_ref, val_ref) = refs[:13], refs[13:15]
    places, scratch = refs[15:26], refs[26:]
    k_ref, v_ref, q_ref, stream_ref, routes_ref, len_ref = places[:6]
    gain_ref, router_ref, fgain_ref, vw_ref, bias_ref = places[6:]
    order = (2, 3, 1, 0, 4, 5, 6, 7, 10, 11, 12)
    wup_ref, wdn_ref = inputs[8], inputs[9]
    (
    wup_v,
    wdn_v,
    kbuf,
    vbuf,
    hid,
    xsend,
    xin,
    xtail_send,
    xtail,
    xall,
    uown,
    usend,
    uin,
    active,
    rsend,
    rin,
    small_send,
    small_in,
    sq_send,
    sq_in,
    wup_sem,
    wdn_sem,
    kv_ss,
    kv_rs,
    x_ss,
    x_rs,
    u_ss,
    u_rs,
    r_ss,
    r_rs,
    s_ss,
    s_rs,
    t_ss,
    t_rs,
    in_sem,
    ) = scratch
    group = lax.axis_index("groups")
    me = lax.axis_index("seq")
    core = lax.axis_index("tp")
    partner = (group, me, 1 - core)
    rows, half = stream_ref.shape
    cap = rows // 2
    owners = n // experts
    up_chunks, up_rows, units = wup_v.shape
    down_chunks, _, down_cols = wdn_v.shape
    part_units = usend.shape[2]
    parts = units // part_units
    kv_heads = k_ref.shape[1] // HD
    per_group = half // HD // kv_heads
    keys = n * rows

    def up_copy(c):
        span = pl.ds(pl.multiple_of(c * up_rows, LANES), up_rows)
        return pltpu.make_async_copy(wup_ref.at[span, :], wup_v.at[c], wup_sem.at[c])

    def down_copy(c):
        cols = pl.ds(pl.multiple_of(c * down_cols, LANES), down_cols)
        return pltpu.make_async_copy(wdn_ref.at[:, cols], wdn_v.at[c], wdn_sem.at[c])

    def peer(step):
        return (group, lax.rem(me + step, n), core)

    barrier = pltpu.get_barrier_semaphore()
    for step in range(1, n):
        pl.semaphore_signal(barrier, inc=1, device_id=peer(step), device_id_type=MESH)
    pl.semaphore_signal(barrier, inc=1, device_id=partner, device_id_type=MESH)
    fetches = [
        pltpu.make_async_copy(inputs[number], place, in_sem.at[spot])
        for spot, (number, place) in enumerate(zip(order, places))
    ]
    for copy in fetches:
        copy.start()
    for copy in fetches:
        copy.wait()
    for c in range(up_chunks):
        up_copy(c).start()
    pl.semaphore_wait(barrier, n)

    sends = []
    for step in range(1, n):
        for which, (own, buf) in enumerate(((k_ref, kbuf), (v_ref, vbuf))):
            copy = remote(own, buf.at[me], kv_ss.at[which, step], kv_rs.at[which, me], peer(step))
            copy.start()
            sends.append(copy)
    for c in range(down_chunks):
        down_copy(c).start()
    kbuf[me] = k_ref[...]
    vbuf[me] = v_ref[...]

    later = lax.broadcasted_iota(jnp.int32, (rows, rows), 0)
    sooner = lax.broadcasted_iota(jnp.int32, (rows, rows), 1)

    def upright(line):
        spread = jnp.where(later == sooner, line.astype(jnp.float32), 0.0)
        return jnp.sum(spread, axis=1, keepdims=True).astype(jnp.int32)

    route0 = upright(routes_ref[0:1, :])
    route1 = upright(routes_ref[1:2, :])
    lower = (sooner < later).astype(jnp.float32).astype(jnp.bfloat16)

    def slots(count, per_expert):
        place = lax.broadcasted_iota(jnp.int32, (rows, count * cap), 1)
        block = block_of(place, cap, count)
        expert = block_of(block, per_expert, experts)
        slot = (place - block * cap).astype(jnp.float32)
        hits = ((route0 == expert) | (route1 == expert)).astype(jnp.float32)
        rank = jnp.dot(lower, hits.astype(jnp.bfloat16), preferred_element_type=jnp.float32)
        return expert, rank == slot

    expert, at_slot = slots(experts, 1)
    placing = (((route0 == expert) | (route1 == expert)) & at_slot).astype(jnp.float32)
    expert_r, at_slot_r = slots(n, owners)
    fetch0 = ((route0 == expert_r) & at_slot_r).astype(jnp.float32)
    fetch1 = ((route1 == expert_r) & at_slot_r).astype(jnp.float32)
    fetch = jnp.concatenate([fetch0, fetch1], axis=0).astype(jnp.bfloat16)

    for step in range(1, n):
        sender = lax.rem(me + n - step, n)
        for which, (own, buf) in enumerate(((k_ref, kbuf), (v_ref, vbuf))):
            remote(
                own, buf.at[sender], kv_ss.at[which, step], kv_rs.at[which, sender], peer(step)
            ).wait_recv()

    inv_root = 1.0 / math.sqrt(HD)
    query_row = lax.broadcasted_iota(jnp.int32, (per_group, rows, keys), 1).reshape(
        per_group * rows, keys
    )
    key_pos = lax.broadcasted_iota(jnp.int32, (per_group * rows, keys), 1)
    allowed = (key_pos <= me * rows + query_row) & (key_pos < len_ref[0])
    for head in range(kv_heads):
        cols = slice(head * HD, (head + 1) * HD)
        k_head = kbuf[:, :, cols].astype(jnp.float32).reshape(keys, HD).astype(jnp.bfloat16)
        v_head = vbuf[:, :, cols].astype(jnp.float32).reshape(keys, HD).astype(jnp.bfloat16)
        base = head * per_group
        q_head = jnp.concatenate(
            [
                q_ref[:, (base + g) * HD : (base + g + 1) * HD].astype(jnp.float32)
                for g in range(per_group)
            ],
            axis=0,
        ).astype(jnp.bfloat16)
        scores = (
            lax.dot_general(
                q_head, k_head, (((1,), (1,)), ((), ())), preferred_element_type=jnp.float32
            )
            * inv_root
        )
        scores = jnp.where(allowed, scores, masked)
        top = jnp.max(scores, axis=-1, keepdims=True)
        weights = jnp.where(allowed, jnp.exp(scores - top), 0.0)
        total = jnp.sum(weights, axis=-1, keepdims=True)
        update = jnp.dot(weights.astype(jnp.bfloat16), v_head, preferred_element_type=jnp.float32)
        update = update / total
        for g in range(per_group):
            out_cols = slice((base + g) * HD, (base + g + 1) * HD)
            hid[:, out_cols] = (
                stream_ref[:, out_cols].astype(jnp.float32) + update[g * rows : (g + 1) * rows]
            )

    hidden = hid[...]
    gained = hidden * gain_ref[...]
    squares = jnp.sum(hidden * hidden, axis=1, keepdims=True)
    lane = lax.broadcasted_iota(jnp.int32, (rows, LANES), 1)

    high = squares.astype(jnp.bfloat16).astype(jnp.float32)
    tail = jnp.where(lane == 0, high, jnp.where(lane == 1, squares - high, 0.0))
    placed = placing.astype(jnp.bfloat16)

    def pack(values):
        return lax.dot_general(
            placed,
            values.astype(jnp.bfloat16),
            (((0,), (0,)), ((), ())),
            preferred_element_type=jnp.float32,
        )

    def dispatch(src_of, dst, send_sem_of, recv_sem):
        for step in range(1, n):
            to = lax.rem(me + step, n)
            copy = remote(
                src_of(to // owners), dst, send_sem_of(step), recv_sem, (group, to, core)
            )
            copy.start()
            sends.append(copy)

    for c in range(up_chunks):
        packed = pack(gained[:, c * up_rows : (c + 1) * up_rows])
        for e in range(experts):
            xsend[c, e] = packed[e * cap : (e + 1) * cap].astype(jnp.bfloat16)
        dispatch(
            lambda e: xsend.at[c, e], xin.at[c, me], lambda step: x_ss.at[c, step], x_rs.at[c, me]
        )
        xin[c, me] = xsend[c, me // owners]
    packed = pack(tail)
    for e in range(experts):
        xtail_send[e] = packed[e * cap : (e + 1) * cap].astype(jnp.bfloat16)
    dispatch(lambda e: xtail_send.at[e], xtail.at[me], lambda step: t_ss.at[step], t_rs.at[me])
    xtail[me] = xtail_send[me // owners]

    stats = jnp.where(lane == experts, squares, 0.0)
    for e in range(experts):
        part = jnp.sum(gained * router_ref[e : e + 1, :], axis=1, keepdims=True)
        stats = jnp.where(lane == e, part, stats)
    small_send[0] = stats
    stat_copy = remote(small_send.at[0], small_in.at[0], s_ss.at[0], s_rs.at[0], partner)
    stat_copy.start()
    sends.append(stat_copy)

    uown[...] = jnp.zeros_like(uown)

    def gather_rows(c):
        for step in range(1, n):
            sender = lax.rem(me + n - step, n)
            remote(
                xsend.at[0, 0], xin.at[c, sender], x_ss.at[c, step], x_rs.at[c, sender], peer(step)
            ).wait_recv()
        arrived = jnp.concatenate([xin[c, d].astype(jnp.float32) for d in range(n)], axis=0)
        xall[...] = arrived.astype(jnp.bfloat16)
        up_copy(c).wait()

    @pl.loop(0, up_chunks - 1)
    def _(c):
        gather_rows(c)
        uown[...] += jnp.dot(xall[...], wup_v[c], preferred_element_type=jnp.float32)

    def exchange(p):
        return remote(usend.at[p], uin.at[p], u_ss.at[p], u_rs.at[p], partner)

    gather_rows(up_chunks - 1)
    for p in range(parts):
        cols = slice(p * part_units, (p + 1) * part_units)
        part = uown[:, cols] + jnp.dot(
            xall[...], wup_v[up_chunks - 1, :, cols], preferred_element_type=jnp.float32
        )
        uown[:, cols] = part
        usend[p] = part.astype(jnp.bfloat16)
        exchange(p).start()
        if p == 0:
            for step in range(1, n):
                sender = lax.rem(me + n - step, n)
                remote(
                    xtail_send.at[0], xtail.at[sender], t_ss.at[step], t_rs.at[sender], peer(step)
                ).wait_recv()
            ends = jnp.concatenate([xtail[d].astype(jnp.float32) for d in range(n)], axis=0)
            sq_send[...] = jnp.broadcast_to(ends[:, 0:1] + ends[:, 1:2], sq_send.shape)
            sq_copy = remote(sq_send, sq_in, s_ss.at[1], s_rs.at[1], partner)
            sq_copy.start()
            sends.append(sq_copy)

    sq_copy.wait_recv()
    scale = lax.rsqrt((sq_send[...] + sq_in[...])[:, 0:1] / width + eps)

    def activate(p):
        exchange(p).wait()
        cols = slice(p * part_units, (p + 1) * part_units)
        up = (uown[:, cols] + uin[p].astype(jnp.float32)) * scale
        active[:, cols] = (up / (1.0 + jnp.exp(-up))).astype(jnp.bfloat16)

    def send_back(c, down):
        for d in range(n):
            rsend[c, d] = down[d * cap : (d + 1) * cap].astype(jnp.bfloat16)
        for step in range(1, n):
            to = lax.rem(me + step, n)
            copy = remote(
                rsend.at[c, to], rin.at[c, me], r_ss.at[c, step], r_rs.at[c, me], (group, to, core)
            )
            copy.start()
            sends.append(copy)
        rin[c, me] = rsend[c, me]

    down = None
    for p in range(parts):
        activate(p)
        if p == 0:
            down_copy(0).wait()
        span = slice(p * part_units, (p + 1) * part_units)
        term = jnp.dot(active[:, span], wdn_v[0, span], preferred_element_type=jnp.float32)
        down = term if down is None else down + term
    send_back(0, down)
    for c in range(1, down_chunks):
        down_copy(c).wait()
        send_back(c, jnp.dot(active[...], wdn_v[c], preferred_element_type=jnp.float32))

    stat_copy.wait_recv()
    both = small_send[0] + small_in[0]
    norm_scale = lax.rsqrt(both[:, experts : experts + 1] / width + eps)
    logits = both * norm_scale
    picked0 = jnp.sum(jnp.where(lane == route0, logits, 0.0), axis=1, keepdims=True)
    picked1 = jnp.sum(jnp.where(lane == route1, logits, 0.0), axis=1, keepdims=True)
    gate0 = 1.0 / (1.0 + jnp.exp(picked1 - picked0))
    gate1 = 1.0 / (1.0 + jnp.exp(picked0 - picked1))

    sq_part = jnp.zeros((rows, 1), jnp.float32)
    dot_part = jnp.zeros((rows, 1), jnp.float32)
    for c in range(down_chunks):
        for step in range(1, n):
            sender = lax.rem(me + n - step, n)
            remote(
                rsend.at[c, 0], rin.at[c, sender], r_ss.at[c, step], r_rs.at[c, sender], peer(step)
            ).wait_recv()
        pieces = jnp.concatenate([rin[c, d].astype(jnp.float32) for d in range(n)], axis=0)
        fetched = jnp.dot(fetch, pieces.astype(jnp.bfloat16), preferred_element_type=jnp.float32)
        cols = slice(c * down_cols, (c + 1) * down_cols)
        final = hid[:, cols] + (gate0 * fetched[:rows] + gate1 * fetched[rows:])
        out_ref[:, cols] = final.astype(jnp.bfloat16)
        sq_part = sq_part + jnp.sum(final * final, axis=1, keepdims=True)
        dot_part = dot_part + jnp.sum(
            final * (fgain_ref[:, cols] * vw_ref[:, cols]), axis=1, keepdims=True
        )
    small_send[1] = jnp.where(lane == 0, sq_part, jnp.where(lane == 1, dot_part, 0.0))
    last = remote(small_send.at[1], small_in.at[1], s_ss.at[2], s_rs.at[2], partner)
    last.start()
    sends.append(last)
    last.wait_recv()
    ends = small_send[1] + small_in[1]
    estimate = ends[:, 1:2] * lax.rsqrt(ends[:, 0:1] / width + eps) + bias_ref[0]
    place = me * rows + lax.broadcasted_iota(jnp.int32, (rows, 1), 0)
    estimate = jnp.where(place < len_ref[0], estimate, 0.0)
    val_ref[...] = jnp.sum(jnp.where(later == sooner, estimate, 0.0), axis=0, keepdims=True)
    for copy in sends:
        copy.wait_send()


def fused(
    stream,
    queries,
    key_rows,
    value_rows,
    routes,
    seq_length,
    norm_gain,
    router,
    w_up,
    w_down,
    final_gain,
    value_weight,
    value_bias,
):
    rows, half = stream.shape
    n = lax.axis_size("seq")
    experts = router.shape[1]
    hidden_units = w_up.shape[1]
    cap = rows // 2
    arrivals = n * cap
    up_rows = largest(half, 768)
    up_chunks = half // up_rows
    down_cols = largest(half, 1024)
    down_chunks = half // down_cols
    part_units = hidden_units // 2
    vmem = pl.BlockSpec(memory_space=pltpu.VMEM)
    hbm = pl.BlockSpec(memory_space=pl.ANY)
    bf16, f32 = jnp.bfloat16, jnp.float32
    dma = pltpu.SemaphoreType.DMA
    out, values = pl.pallas_call(
        functools.partial(layer_kernel, n, experts, half * lax.axis_size("tp")),
        out_shape=(
            jax.ShapeDtypeStruct((rows, half), bf16),
            jax.ShapeDtypeStruct((1, rows), f32),
        ),
        in_specs=[hbm] * 13,
        out_specs=(vmem, vmem),
        scratch_shapes=[
            pltpu.VMEM(key_rows.shape, bf16),
            pltpu.VMEM(key_rows.shape, bf16),
            pltpu.VMEM(stream.shape, bf16),
            pltpu.VMEM(stream.shape, bf16),
            pltpu.VMEM((2, rows), jnp.int32),
            pltpu.SMEM((1,), jnp.int32),
            pltpu.VMEM((1, half), f32),
            pltpu.VMEM((experts, half), f32),
            pltpu.VMEM((1, half), f32),
            pltpu.VMEM((1, half), f32),
            pltpu.SMEM((1,), f32),
            pltpu.VMEM((up_chunks, up_rows, hidden_units), bf16),
            pltpu.VMEM((down_chunks, hidden_units, down_cols), bf16),
            pltpu.VMEM((n, rows, key_rows.shape[1]), bf16),
            pltpu.VMEM((n, rows, key_rows.shape[1]), bf16),
            pltpu.VMEM((rows, half), f32),
            pltpu.VMEM((up_chunks, experts, cap, up_rows), bf16),
            pltpu.VMEM((up_chunks, n, cap, up_rows), bf16),
            pltpu.VMEM((experts, cap, LANES), bf16),
            pltpu.VMEM((n, cap, LANES), bf16),
            pltpu.VMEM((arrivals, up_rows), bf16),
            pltpu.VMEM((arrivals, hidden_units), f32),
            pltpu.VMEM((2, arrivals, part_units), bf16),
            pltpu.VMEM((2, arrivals, part_units), bf16),
            pltpu.VMEM((arrivals, hidden_units), bf16),
            pltpu.VMEM((down_chunks, n, cap, down_cols), bf16),
            pltpu.VMEM((down_chunks, n, cap, down_cols), bf16),
            pltpu.VMEM((2, rows, LANES), f32),
            pltpu.VMEM((2, rows, LANES), f32),
            pltpu.VMEM((arrivals, LANES), f32),
            pltpu.VMEM((arrivals, LANES), f32),
            dma((up_chunks,)),
            dma((down_chunks,)),
            dma((2, n)),
            dma((2, n)),
            dma((up_chunks, n)),
            dma((up_chunks, n)),
            dma((2,)),
            dma((2,)),
            dma((down_chunks, n)),
            dma((down_chunks, n)),
            dma((3,)),
            dma((3,)),
            dma((n,)),
            dma((n,)),
            dma((11,)),
        ],
        compiler_params=pltpu.CompilerParams(
            collective_id=0, has_side_effects=True, vmem_limit_bytes=VMEM_BYTES
        ),
        name="layer",
    )(
        stream,
        queries,
        key_rows,
        value_rows,
        routes.T,
        seq_length,
        norm_gain.reshape(1, half),
        router.T,
        w_up,
        w_down,
        final_gain.reshape(1, half),
        value_weight.reshape(1, half),
        value_bias,
    )
    return out, values.reshape(rows)


def unfused(
    stream,
    queries,
    key_rows,
    value_rows,
    routes,
    seq_length,
    norm_gain,
    router,
    w_up,
    w_down,
    final_gain,
    value_weight,
    value_bias,
):
    row_count = stream.shape[0]
    half_width = stream.shape[1]
    width = half_width * lax.axis_size("tp")
    experts = router.shape[1]
    seq_devices = lax.axis_size("seq")
    owners = seq_devices // experts
    my_index = lax.axis_index("seq")
    seq_limit = seq_length[0]
    positions = my_index * row_count + jnp.arange(row_count, dtype=jnp.int32)
    kv_heads = key_rows.shape[1] // HD
    per_group = queries.shape[1] // HD // kv_heads
    grouped = queries.reshape(row_count, kv_heads, per_group, HD)
    inv_root = 1.0 / math.sqrt(HD)
    slot_cap = row_count // 2
    run_max = jnp.full((kv_heads, per_group, row_count), masked, jnp.float32)
    key_block = lax.all_gather(key_rows, "seq", axis=0, tiled=True)
    value_block = lax.all_gather(value_rows, "seq", axis=0, tiled=True)
    key_count = key_block.shape[0]
    scores = (
        jnp.einsum(
            "qkgd,ckd->kgqc",
            grouped,
            key_block.reshape(key_count, kv_heads, HD),
            preferred_element_type=jnp.float32,
        )
        * inv_root
    )
    key_pos = jnp.arange(key_count, dtype=jnp.int32)
    allowed = (key_pos[None, :] <= positions[:, None]) & (key_pos[None, :] < seq_limit)
    scores = jnp.where(allowed, scores, masked)
    new_max = jnp.maximum(run_max, jnp.max(scores, axis=-1))
    weights = jnp.where(allowed, jnp.exp(scores - new_max[..., None]), 0.0)
    new_sum = jnp.sum(weights, axis=-1)
    update = jnp.einsum(
        "kgqc,ckd->kgqd",
        weights.astype(jnp.bfloat16),
        value_block.reshape(key_count, kv_heads, HD),
        preferred_element_type=jnp.float32,
    )
    attended = (update / new_sum[..., None]).transpose(2, 0, 1, 3).reshape(row_count, half_width)
    hidden = stream.astype(jnp.float32) + attended
    gained = hidden * norm_gain
    squares = jnp.sum(hidden * hidden, axis=1)
    total_sq = lax.psum(squares, "tp")
    norm_scale = lax.rsqrt(total_sq / width + eps)
    normed = gained * norm_scale[:, None]
    logits = lax.psum(jnp.dot(normed, router, precision=lax.Precision.HIGHEST), "tp")
    normed_half = normed.astype(jnp.bfloat16)
    expert_ids = jnp.arange(experts, dtype=jnp.int32)
    chosen = (routes[:, :, None] == expert_ids).astype(jnp.float32)
    picked = jnp.sum(chosen * logits[:, None, :], axis=2)
    gates = jax.nn.sigmoid(picked - picked[:, ::-1])
    flat_hits = chosen.reshape(row_count * 2, experts)
    earlier = jnp.cumsum(flat_hits, axis=0) - flat_hits
    slot_index = jnp.sum(earlier * flat_hits, axis=1).astype(jnp.int32)
    target = routes.reshape(row_count * 2) * slot_cap + slot_index
    placing = (target[:, None] == jnp.arange(experts * slot_cap, dtype=jnp.int32)[None, :]).astype(
        jnp.bfloat16
    )
    doubled = jnp.repeat(normed_half, 2, axis=0)
    packed = jnp.einsum("pe,pd->ed", placing, doubled, preferred_element_type=jnp.float32).astype(
        jnp.bfloat16
    )
    outgoing = jnp.broadcast_to(
        packed.reshape(experts, 1, slot_cap, half_width), (experts, owners, slot_cap, half_width)
    ).reshape(seq_devices, slot_cap, half_width)
    arrived = lax.all_to_all(outgoing, "seq", split_axis=0, concat_axis=0, tiled=True)
    lead = arrived.shape[0]
    items = arrived.shape[1]
    flat_rows = arrived.reshape(lead * items, half_width)
    up_part = jnp.dot(flat_rows, w_up, preferred_element_type=jnp.float32)
    up_total = lax.psum(up_part.astype(jnp.bfloat16), "tp").astype(jnp.float32)
    active = jax.nn.silu(up_total).astype(jnp.bfloat16)
    down_part = jnp.dot(active, w_down, preferred_element_type=jnp.float32).astype(jnp.bfloat16)
    partial_out = down_part.reshape(lead, items, half_width)
    returned = lax.all_to_all(partial_out, "seq", split_axis=0, concat_axis=0, tiled=True)
    summed = jnp.sum(
        returned.reshape(experts, owners, slot_cap, half_width), axis=1, dtype=jnp.float32
    ).reshape(experts * slot_cap, half_width)
    fetched = jnp.dot(placing.astype(jnp.float32), summed, precision=lax.Precision.HIGHEST)
    mixed = jnp.sum(fetched.reshape(row_count, 2, half_width) * gates[:, :, None], axis=1)
    final = hidden + mixed
    sq_part = jnp.sum(final * final, axis=1)
    dot_part = jnp.sum(final * (final_gain * value_weight), axis=1)
    sq_total, dot_total = lax.psum((sq_part, dot_part), "tp")
    estimate = dot_total * lax.rsqrt(sq_total / width + eps) + value_bias[0]
    estimate = jnp.where(positions < seq_limit, estimate, 0.0)
    return (final.astype(jnp.bfloat16), estimate)


def on_device(*args):
    stream, w_up = args[0], args[8]
    arrivals = lax.axis_size("seq") * (stream.shape[0] // 2)
    weight_bytes = 4 * w_up.shape[0] * w_up.shape[1]
    small = arrivals <= ROW_LIMIT and weight_bytes <= 52 * 1024 * 1024
    return fused(*args) if small else unfused(*args)


def solution(mesh):
    return jax.shard_map(
        on_device,
        mesh=mesh,
        in_specs=(
            P(("groups", "seq"), "tp"),
            P(("groups", "seq"), "tp"),
            P(("groups", "seq"), "tp"),
            P(("groups", "seq"), "tp"),
            P(("groups", "seq"), None),
            P("groups"),
            P("tp"),
            P("tp", None),
            P("tp", "seq"),
            P("seq", "tp"),
            P("tp"),
            P("tp"),
            P(),
        ),
        out_specs=(P(("groups", "seq"), "tp"), P(("groups", "seq"))),
        check_vma=False,
    )
```

profile of v0, /device:TPU:1, one launch (start us, length us, event | category | flops | bytes accessed | tf_op | source)
XLA Modules:
  0.0 38.0 jit_solution(7078721386555805497)
XLA Ops:
  1.9 33.5 %layer.1 = (bf16[8,3072]{1,0:T(8,128)(2,1)}, f32[1,8]{1,0:T(1,128)}) custom-call(bf16[8,3072]{1,0:T(8,128)(2,1)} %refs_0_.1, bf16[8,3072]{1,0:T(8,128)(2,1)} %refs_1_.1, bf16[8,512]{1,0:T(8,128)(2,1)} %refs_2_.1, bf16[8,512]{1,0:T(8,128)(2,1)} %refs_3_.1, s32[2,8]{1,0:T(2,128)} %bitcast.10, s32[1]{0:T(128)S(6)} %copy.17.refs_5_, f32[1,3072]{1,0:T(1,128)} %bitcast.7, ...), custom_call_target="tpu_custom_call" | custom-call | tf_op jit(solution)/shard_map/layer/pallas_call | solution.py:410
  35.4 1.4 %copy.19 = bf16[8,3072]{1,0:T(8,128)(2,1)} copy(bf16[8,3072]{1,0:T(8,128)(2,1)} %get-tuple-element.8) | data formatting | bytes 98304
  36.9 1.1 %copy.20 = f32[8]{0:T(128)} copy(f32[8]{0:T(128)} %bitcast.11) | data formatting | bytes 64
where the time goes:
time: 38.3 us; the launch traced here: 38 us
  Pallas kernels  33.5 us (87%)
  local copies, waits for them, and re-layouts  2.57 us (7%)
  between operations  1.93 us (5%)
    pallas_call x1, Pallas kernels, fused(): pl.pallas_call(functools.partial(layer_kernel, n, experts, half * lax.axi...  33.5 us
    unnamed x2, local copies, waits for them, and re-layouts  2.57 us

commit v1 on v0

--- a/solution.py
+++ b/solution.py
@@ -130,6 +130,8 @@
         copy.wait()
     for c in range(up_chunks):
         up_copy(c).start()
+    for c in range(down_chunks):
+        down_copy(c).start()
     pl.semaphore_wait(barrier, n)
 
     sends = []
@@ -138,8 +140,6 @@
             copy = remote(own, buf.at[me], kv_ss.at[which, step], kv_rs.at[which, me], peer(step))
             copy.start()
             sends.append(copy)
-    for c in range(down_chunks):
-        down_copy(c).start()
     kbuf[me] = k_ref[...]
     vbuf[me] = v_ref[...]
 
@@ -377,6 +377,17 @@
         copy.wait_send()
 
 
+def store_kernel(out_ref, val_ref, out_hbm, val_hbm, sem):
+    copies = [
+        pltpu.make_async_copy(out_ref, out_hbm, sem.at[0]),
+        pltpu.make_async_copy(val_ref, val_hbm, sem.at[1]),
+    ]
+    for copy in copies:
+        copy.start()
+    for copy in copies:
+        copy.wait()
+
+
 def fused(
     stream,
     queries,
@@ -404,15 +415,13 @@
     down_chunks = half // down_cols
     part_units = hidden_units // 2
     vmem = pl.BlockSpec(memory_space=pltpu.VMEM)
-    hbm = pl.BlockSpec(memory_space=pl.ANY)
+    hbm = pl.BlockSpec(memory_space=pltpu.HBM)
+    raw = pl.BlockSpec(memory_space=pl.ANY)
     bf16, f32 = jnp.bfloat16, jnp.float32
     dma = pltpu.SemaphoreType.DMA
     out, values = pl.pallas_call(
         functools.partial(layer_kernel, n, experts, half * lax.axis_size("tp")),
-        out_shape=(
-            jax.ShapeDtypeStruct((rows, half), bf16),
-            jax.ShapeDtypeStruct((1, rows), f32),
-        ),
+        out_shape=(pltpu.VMEM((rows, half), bf16), pltpu.VMEM((1, rows), f32)),
         in_specs=[hbm] * 13,
         out_specs=(vmem, vmem),
         scratch_shapes=[
@@ -482,6 +491,20 @@
         value_weight.reshape(1, half),
         value_bias,
     )
+    out, values = pl.pallas_call(
+        store_kernel,
+        out_shape=(
+            jax.ShapeDtypeStruct((rows, half), bf16),
+            jax.ShapeDtypeStruct((1, rows), f32),
+        ),
+        in_specs=[raw, raw],
+        out_specs=(hbm, hbm),
+        scratch_shapes=[dma((2,))],
+        name="store",
+    )(
+        pltpu.with_memory_space_constraint(out, pltpu.VMEM),
+        pltpu.with_memory_space_constraint(values, pltpu.VMEM),
+    )
     return out, values.reshape(rows)
 
 

time: 38.3 us -> 35.7 us (0.932)
  local copies, waits for them, and re-layouts: 2.57 us -> 0 us
    unnamed x2 -> x0, local copies, waits for them, and re-layouts: 2.57 us -> none
    pallas_call x0 -> x1, Pallas kernels: none -> 0.64 us  [fused(): pl.pallas_call(store_kernel, out_shape=(jax.ShapeDtypeStruct((rows, half)...]
    pallas_call x1, Pallas kernels: 33.5 us -> 32.9 us  [fused(): pl.pallas_call(functools.partial(layer_kernel, n, experts, half * lax.axi...]
where the time goes in v1:
time: 35.7 us; the launch traced here: 35.5 us
  Pallas kernels  33.5 us (94%)
  between operations  1.93 us (5%)
    pallas_call x1, Pallas kernels, fused(): pl.pallas_call(functools.partial(layer_kernel, n, experts, half * lax.axi...  32.9 us

profile of v1, /device:TPU:1, one launch (start us, length us, event | category | flops | bytes accessed | tf_op | source)
XLA Modules:
  0.0 35.5 jit_solution(2230947652506568443)
XLA Ops:
  1.9 32.9 %layer.1 = (bf16[8,3072]{1,0:T(8,128)(2,1)S(1)}, f32[1,8]{1,0:T(1,128)S(1)}) custom-call(bf16[8,3072]{1,0:T(8,128)(2,1)} %refs_0_.1, bf16[8,3072]{1,0:T(8,128)(2,1)} %refs_1_.1, bf16[8,512]{1,0:T(8,128)(2,1)} %refs_2_.1, bf16[8,512]{1,0:T(8,128)(2,1)} %refs_3_.1, s32[2,8]{1,0:T(2,128)} %bitcast.10, s32[1]{0:T(128)S(6)} %copy.15.refs_5_, f32[1,3072]{1,0:T(1,128)} %bitcast.7, ...), custom_call_target="tpu_custom_call" | custom-call | tf_op jit(solution)/shard_map/layer/pallas_call | solution.py:422
  34.8 0.6 %store.1 = (bf16[8,3072]{1,0:T(8,128)(2,1)}, f32[1,8]{1,0:T(1,128)}) custom-call(bf16[8,3072]{1,0:T(8,128)(2,1)S(1)} %get-tuple-element.6.out_ref, f32[1,8]{1,0:T(1,128)S(1)} %get-tuple-element.7.val_ref), custom_call_target="tpu_custom_call" | custom-call | tf_op jit(solution)/shard_map/store/pallas_call | solution.py:494

commit v2 on v1

--- a/solution.py
+++ b/solution.py
@@ -48,16 +48,15 @@
     *refs,
 ):
     inputs, (out_ref, val_ref) = refs[:13], refs[13:15]
-    places, scratch = refs[15:26], refs[26:]
-    k_ref, v_ref, q_ref, stream_ref, routes_ref, len_ref = places[:6]
-    gain_ref, router_ref, fgain_ref, vw_ref, bias_ref = places[6:]
-    order = (2, 3, 1, 0, 4, 5, 6, 7, 10, 11, 12)
+    places, scratch = refs[15:24], refs[24:]
+    q_ref, stream_ref, routes_ref, len_ref = places[:4]
+    gain_ref, router_ref, fgain_ref, vw_ref, bias_ref = places[4:]
+    order = (1, 0, 4, 5, 6, 7, 10, 11, 12)
     wup_ref, wdn_ref = inputs[8], inputs[9]
     (
     wup_v,
     wdn_v,
-    kbuf,
-    vbuf,
+    kvbuf,
     hid,
     xsend,
     xin,
@@ -99,11 +98,11 @@
     owners = n // experts
     up_chunks, up_rows, units = wup_v.shape
     down_chunks, _, down_cols = wdn_v.shape
-    part_units = usend.shape[2]
-    parts = units // part_units
-    kv_heads = k_ref.shape[1] // HD
+    parts, _, part_units = usend.shape
+    kv_heads = kvbuf.shape[3] // HD
     per_group = half // HD // kv_heads
     keys = n * rows
+    others = pl.ds(0, n - 1)
 
     def up_copy(c):
         span = pl.ds(pl.multiple_of(c * up_rows, LANES), up_rows)
@@ -113,15 +112,21 @@
         cols = pl.ds(pl.multiple_of(c * down_cols, LANES), down_cols)
         return pltpu.make_async_copy(wdn_ref.at[:, cols], wdn_v.at[c], wdn_sem.at[c])
 
-    def peer(step):
-        return (group, lax.rem(me + step, n), core)
-
+    def other(step):
+        return step + (step >= me).astype(jnp.int32)
+
+    kvbuf[...] = jnp.zeros_like(kvbuf)
     barrier = pltpu.get_barrier_semaphore()
-    for step in range(1, n):
-        pl.semaphore_signal(barrier, inc=1, device_id=peer(step), device_id_type=MESH)
+    for step in range(n - 1):
+        pl.semaphore_signal(
+            barrier, inc=1, device_id=(group, other(step), core), device_id_type=MESH
+        )
     pl.semaphore_signal(barrier, inc=1, device_id=partner, device_id_type=MESH)
     fetches = [
-        pltpu.make_async_copy(inputs[number], place, in_sem.at[spot])
+        pltpu.make_async_copy(inputs[2 + which], kvbuf.at[me, which], in_sem.at[which])
+        for which in range(2)
+    ] + [
+        pltpu.make_async_copy(inputs[number], place, in_sem.at[2 + spot])
         for spot, (number, place) in enumerate(zip(order, places))
     ]
     for copy in fetches:
@@ -130,18 +135,18 @@
         copy.wait()
     for c in range(up_chunks):
         up_copy(c).start()
-    for c in range(down_chunks):
-        down_copy(c).start()
     pl.semaphore_wait(barrier, n)
 
-    sends = []
-    for step in range(1, n):
-        for which, (own, buf) in enumerate(((k_ref, kbuf), (v_ref, vbuf))):
-            copy = remote(own, buf.at[me], kv_ss.at[which, step], kv_rs.at[which, me], peer(step))
-            copy.start()
-            sends.append(copy)
-    kbuf[me] = k_ref[...]
-    vbuf[me] = v_ref[...]
+    def kv_copy(block, step, to):
+        return remote(
+            kvbuf.at[block], kvbuf.at[block], kv_ss.at[step], kv_rs.at[block], (group, to, core)
+        )
+
+    for step in range(n - 1, 0, -1):
+
+        @pl.when(me + step < n)
+        def _(step=step):
+            kv_copy(me, step, lax.rem(me + step, n)).start()
 
     later = lax.broadcasted_iota(jnp.int32, (rows, rows), 0)
     sooner = lax.broadcasted_iota(jnp.int32, (rows, rows), 1)
@@ -165,17 +170,33 @@
 
     expert, at_slot = slots(experts, 1)
     placing = (((route0 == expert) | (route1 == expert)) & at_slot).astype(jnp.float32)
+    placed = placing.astype(jnp.bfloat16)
     expert_r, at_slot_r = slots(n, owners)
     fetch0 = ((route0 == expert_r) & at_slot_r).astype(jnp.float32)
     fetch1 = ((route1 == expert_r) & at_slot_r).astype(jnp.float32)
     fetch = jnp.concatenate([fetch0, fetch1], axis=0).astype(jnp.bfloat16)
 
-    for step in range(1, n):
-        sender = lax.rem(me + n - step, n)
-        for which, (own, buf) in enumerate(((k_ref, kbuf), (v_ref, vbuf))):
-            remote(
-                own, buf.at[sender], kv_ss.at[which, step], kv_rs.at[which, sender], peer(step)
-            ).wait_recv()
+    for step in range(n - 1, 0, -1):
+
+        @pl.when(step <= me)
+        def _(step=step):
+            kv_copy(lax.rem(me + n - step, n), step, me).wait_recv()
+
+    for c in range(down_chunks):
+        down_copy(c).start()
+
+    def pack(values):
+        return lax.dot_general(
+            placed,
+            values.astype(jnp.bfloat16),
+            (((0,), (0,)), ((), ())),
+            preferred_element_type=jnp.float32,
+        )
+
+    def dispatch(src_of, dst, send_sem, recv_sem):
+        for step in range(n - 1):
+            to = other(step)
+            remote(src_of(to // owners), dst, send_sem, recv_sem, (group, to, core)).start()
 
     inv_root = 1.0 / math.sqrt(HD)
     query_row = lax.broadcasted_iota(jnp.int32, (per_group, rows, keys), 1).reshape(
@@ -183,10 +204,10 @@
     )
     key_pos = lax.broadcasted_iota(jnp.int32, (per_group * rows, keys), 1)
     allowed = (key_pos <= me * rows + query_row) & (key_pos < len_ref[0])
+    all_scores = []
     for head in range(kv_heads):
         cols = slice(head * HD, (head + 1) * HD)
-        k_head = kbuf[:, :, cols].astype(jnp.float32).reshape(keys, HD).astype(jnp.bfloat16)
-        v_head = vbuf[:, :, cols].astype(jnp.float32).reshape(keys, HD).astype(jnp.bfloat16)
+        k_head = kvbuf[:, 0, :, cols].astype(jnp.float32).reshape(keys, HD).astype(jnp.bfloat16)
         base = head * per_group
         q_head = jnp.concatenate(
             [
@@ -195,94 +216,82 @@
             ],
             axis=0,
         ).astype(jnp.bfloat16)
-        scores = (
+        all_scores.append(
             lax.dot_general(
                 q_head, k_head, (((1,), (1,)), ((), ())), preferred_element_type=jnp.float32
             )
             * inv_root
         )
-        scores = jnp.where(allowed, scores, masked)
+    updates = []
+    for head in range(kv_heads):
+        cols = slice(head * HD, (head + 1) * HD)
+        v_head = kvbuf[:, 1, :, cols].astype(jnp.float32).reshape(keys, HD).astype(jnp.bfloat16)
+        scores = jnp.where(allowed, all_scores[head], masked)
         top = jnp.max(scores, axis=-1, keepdims=True)
         weights = jnp.where(allowed, jnp.exp(scores - top), 0.0)
         total = jnp.sum(weights, axis=-1, keepdims=True)
         update = jnp.dot(weights.astype(jnp.bfloat16), v_head, preferred_element_type=jnp.float32)
-        update = update / total
-        for g in range(per_group):
-            out_cols = slice((base + g) * HD, (base + g + 1) * HD)
-            hid[:, out_cols] = (
-                stream_ref[:, out_cols].astype(jnp.float32) + update[g * rows : (g + 1) * rows]
-            )
-
-    hidden = hid[...]
-    gained = hidden * gain_ref[...]
-    squares = jnp.sum(hidden * hidden, axis=1, keepdims=True)
+        updates.append(update / total)
+    squares = jnp.zeros((rows, 1), jnp.float32)
+    chunks = []
+    for c in range(up_chunks):
+        span = slice(c * up_rows, (c + 1) * up_rows)
+        update = jnp.concatenate(
+            [updates[c][g * rows : (g + 1) * rows] for g in range(per_group)], axis=1
+        )
+        hidden = stream_ref[:, span].astype(jnp.float32) + update
+        hid[:, span] = hidden
+        gained = hidden * gain_ref[:, span]
+        chunks.append(gained)
+        squares = squares + jnp.sum(hidden * hidden, axis=1, keepdims=True)
+        packed = pack(gained)
+        for e in range(experts):
+            xsend[c, e] = packed[e * cap : (e + 1) * cap].astype(jnp.bfloat16)
+        dispatch(lambda e: xsend.at[c, e], xin.at[c, me], x_ss.at[0], x_rs.at[c])
+        xin[c, me] = xsend[c, me // owners]
     lane = lax.broadcasted_iota(jnp.int32, (rows, LANES), 1)
-
     high = squares.astype(jnp.bfloat16).astype(jnp.float32)
     tail = jnp.where(lane == 0, high, jnp.where(lane == 1, squares - high, 0.0))
-    placed = placing.astype(jnp.bfloat16)
-
-    def pack(values):
-        return lax.dot_general(
-            placed,
-            values.astype(jnp.bfloat16),
-            (((0,), (0,)), ((), ())),
-            preferred_element_type=jnp.float32,
-        )
-
-    def dispatch(src_of, dst, send_sem_of, recv_sem):
-        for step in range(1, n):
-            to = lax.rem(me + step, n)
-            copy = remote(
-                src_of(to // owners), dst, send_sem_of(step), recv_sem, (group, to, core)
-            )
-            copy.start()
-            sends.append(copy)
-
-    for c in range(up_chunks):
-        packed = pack(gained[:, c * up_rows : (c + 1) * up_rows])
-        for e in range(experts):
-            xsend[c, e] = packed[e * cap : (e + 1) * cap].astype(jnp.bfloat16)
-        dispatch(
-            lambda e: xsend.at[c, e], xin.at[c, me], lambda step: x_ss.at[c, step], x_rs.at[c, me]
-        )
-        xin[c, me] = xsend[c, me // owners]
     packed = pack(tail)
     for e in range(experts):
         xtail_send[e] = packed[e * cap : (e + 1) * cap].astype(jnp.bfloat16)
-    dispatch(lambda e: xtail_send.at[e], xtail.at[me], lambda step: t_ss.at[step], t_rs.at[me])
+    dispatch(lambda e: xtail_send.at[e], xtail.at[me], t_ss.at[0], t_rs.at[0])
     xtail[me] = xtail_send[me // owners]
 
     stats = jnp.where(lane == experts, squares, 0.0)
     for e in range(experts):
-        part = jnp.sum(gained * router_ref[e : e + 1, :], axis=1, keepdims=True)
+        part = jnp.zeros((rows, 1), jnp.float32)
+        for c in range(up_chunks):
+            weight = router_ref[e : e + 1, c * up_rows : (c + 1) * up_rows]
+            part = part + jnp.sum(chunks[c] * weight, axis=1, keepdims=True)
         stats = jnp.where(lane == e, part, stats)
     small_send[0] = stats
     stat_copy = remote(small_send.at[0], small_in.at[0], s_ss.at[0], s_rs.at[0], partner)
     stat_copy.start()
-    sends.append(stat_copy)
-
-    uown[...] = jnp.zeros_like(uown)
+
+    def arrival(block, recv_sem):
+        return remote(block, block, x_ss.at[0], recv_sem, partner)
 
     def gather_rows(c):
-        for step in range(1, n):
-            sender = lax.rem(me + n - step, n)
-            remote(
-                xsend.at[0, 0], xin.at[c, sender], x_ss.at[c, step], x_rs.at[c, sender], peer(step)
-            ).wait_recv()
+        arrival(xin.at[c, others], x_rs.at[c]).wait_recv()
         arrived = jnp.concatenate([xin[c, d].astype(jnp.float32) for d in range(n)], axis=0)
-        xall[...] = arrived.astype(jnp.bfloat16)
         up_copy(c).wait()
-
-    @pl.loop(0, up_chunks - 1)
-    def _(c):
-        gather_rows(c)
-        uown[...] += jnp.dot(xall[...], wup_v[c], preferred_element_type=jnp.float32)
+        return arrived.astype(jnp.bfloat16)
 
     def exchange(p):
         return remote(usend.at[p], uin.at[p], u_ss.at[p], u_rs.at[p], partner)
 
-    gather_rows(up_chunks - 1)
+    for c in range(up_chunks - 1):
+        xall[...] = gather_rows(c)
+        term = jnp.dot(xall[...], wup_v[c], preferred_element_type=jnp.float32)
+        uown[...] = term if c == 0 else uown[...] + term
+
+    xall[...] = gather_rows(up_chunks - 1)
+    arrival(xtail.at[others], t_rs.at[0]).wait_recv()
+    ends = jnp.concatenate([xtail[d].astype(jnp.float32) for d in range(n)], axis=0)
+    sq_send[...] = jnp.broadcast_to(ends[:, 0:1] + ends[:, 1:2], sq_send.shape)
+    sq_copy = remote(sq_send, sq_in, s_ss.at[1], s_rs.at[1], partner)
+    sq_copy.start()
     for p in range(parts):
         cols = slice(p * part_units, (p + 1) * part_units)
         part = uown[:, cols] + jnp.dot(
@@ -291,23 +300,12 @@
         uown[:, cols] = part
         usend[p] = part.astype(jnp.bfloat16)
         exchange(p).start()
-        if p == 0:
-            for step in range(1, n):
-                sender = lax.rem(me + n - step, n)
-                remote(
-                    xtail_send.at[0], xtail.at[sender], t_ss.at[step], t_rs.at[sender], peer(step)
-                ).wait_recv()
-            ends = jnp.concatenate([xtail[d].astype(jnp.float32) for d in range(n)], axis=0)
-            sq_send[...] = jnp.broadcast_to(ends[:, 0:1] + ends[:, 1:2], sq_send.shape)
-            sq_copy = remote(sq_send, sq_in, s_ss.at[1], s_rs.at[1], partner)
-            sq_copy.start()
-            sends.append(sq_copy)
 
     sq_copy.wait_recv()
     scale = lax.rsqrt((sq_send[...] + sq_in[...])[:, 0:1] / width + eps)
 
     def activate(p):
-        exchange(p).wait()
+        exchange(p).wait_recv()
         cols = slice(p * part_units, (p + 1) * part_units)
         up = (uown[:, cols] + uin[p].astype(jnp.float32)) * scale
         active[:, cols] = (up / (1.0 + jnp.exp(-up))).astype(jnp.bfloat16)
@@ -315,25 +313,26 @@
     def send_back(c, down):
         for d in range(n):
             rsend[c, d] = down[d * cap : (d + 1) * cap].astype(jnp.bfloat16)
-        for step in range(1, n):
-            to = lax.rem(me + step, n)
-            copy = remote(
-                rsend.at[c, to], rin.at[c, me], r_ss.at[c, step], r_rs.at[c, me], (group, to, core)
-            )
-            copy.start()
-            sends.append(copy)
+        for step in range(n - 1):
+            to = other(step)
+            remote(
+                rsend.at[c, to], rin.at[c, me], r_ss.at[0], r_rs.at[c], (group, to, core)
+            ).start()
         rin[c, me] = rsend[c, me]
 
-    down = None
+    first = min(2, down_chunks)
+    downs = [None] * first
     for p in range(parts):
         activate(p)
-        if p == 0:
-            down_copy(0).wait()
         span = slice(p * part_units, (p + 1) * part_units)
-        term = jnp.dot(active[:, span], wdn_v[0, span], preferred_element_type=jnp.float32)
-        down = term if down is None else down + term
-    send_back(0, down)
-    for c in range(1, down_chunks):
+        for c in range(first):
+            if p == 0:
+                down_copy(c).wait()
+            term = jnp.dot(active[:, span], wdn_v[c, span], preferred_element_type=jnp.float32)
+            downs[c] = term if p == 0 else downs[c] + term
+    for c in range(first):
+        send_back(c, downs[c])
+    for c in range(first, down_chunks):
         down_copy(c).wait()
         send_back(c, jnp.dot(active[...], wdn_v[c], preferred_element_type=jnp.float32))
 
@@ -349,11 +348,7 @@
     sq_part = jnp.zeros((rows, 1), jnp.float32)
     dot_part = jnp.zeros((rows, 1), jnp.float32)
     for c in range(down_chunks):
-        for step in range(1, n):
-            sender = lax.rem(me + n - step, n)
-            remote(
-                rsend.at[c, 0], rin.at[c, sender], r_ss.at[c, step], r_rs.at[c, sender], peer(step)
-            ).wait_recv()
+        arrival(rin.at[c, others], r_rs.at[c]).wait_recv()
         pieces = jnp.concatenate([rin[c, d].astype(jnp.float32) for d in range(n)], axis=0)
         fetched = jnp.dot(fetch, pieces.astype(jnp.bfloat16), preferred_element_type=jnp.float32)
         cols = slice(c * down_cols, (c + 1) * down_cols)
@@ -366,15 +361,30 @@
     small_send[1] = jnp.where(lane == 0, sq_part, jnp.where(lane == 1, dot_part, 0.0))
     last = remote(small_send.at[1], small_in.at[1], s_ss.at[2], s_rs.at[2], partner)
     last.start()
-    sends.append(last)
+
+    def sent(block, send_sem):
+        remote(block, block, send_sem, r_rs.at[0], partner).wait_send()
+
+    for step in range(1, n):
+
+        @pl.when(me + step < n)
+        def _(step=step):
+            kv_copy(me, step, me).wait_send()
+
+    sent(xin.at[:, others], x_ss.at[0])
+    sent(xtail.at[others], t_ss.at[0])
+    sent(rin.at[:, others], r_ss.at[0])
+    for p in range(parts):
+        exchange(p).wait_send()
+    stat_copy.wait_send()
+    sq_copy.wait_send()
     last.wait_recv()
     ends = small_send[1] + small_in[1]
     estimate = ends[:, 1:2] * lax.rsqrt(ends[:, 0:1] / width + eps) + bias_ref[0]
     place = me * rows + lax.broadcasted_iota(jnp.int32, (rows, 1), 0)
     estimate = jnp.where(place < len_ref[0], estimate, 0.0)
     val_ref[...] = jnp.sum(jnp.where(later == sooner, estimate, 0.0), axis=0, keepdims=True)
-    for copy in sends:
-        copy.wait_send()
+    last.wait_send()
 
 
 def store_kernel(out_ref, val_ref, out_hbm, val_hbm, sem):
@@ -409,11 +419,13 @@
     hidden_units = w_up.shape[1]
     cap = rows // 2
     arrivals = n * cap
-    up_rows = largest(half, 768)
-    up_chunks = half // up_rows
-    down_cols = largest(half, 1024)
+    kv_cols = key_rows.shape[1]
+    up_chunks = kv_cols // HD
+    up_rows = half // up_chunks
+    down_cols = largest(half, 512)
     down_chunks = half // down_cols
-    part_units = hidden_units // 2
+    parts = 4
+    part_units = hidden_units // parts
     vmem = pl.BlockSpec(memory_space=pltpu.VMEM)
     hbm = pl.BlockSpec(memory_space=pltpu.HBM)
     raw = pl.BlockSpec(memory_space=pl.ANY)
@@ -425,8 +437,6 @@
         in_specs=[hbm] * 13,
         out_specs=(vmem, vmem),
         scratch_shapes=[
-            pltpu.VMEM(key_rows.shape, bf16),
-            pltpu.VMEM(key_rows.shape, bf16),
             pltpu.VMEM(stream.shape, bf16),
             pltpu.VMEM(stream.shape, bf16),
             pltpu.VMEM((2, rows), jnp.int32),
@@ -438,8 +448,7 @@
             pltpu.SMEM((1,), f32),
             pltpu.VMEM((up_chunks, up_rows, hidden_units), bf16),
             pltpu.VMEM((down_chunks, hidden_units, down_cols), bf16),
-            pltpu.VMEM((n, rows, key_rows.shape[1]), bf16),
-            pltpu.VMEM((n, rows, key_rows.shape[1]), bf16),
+            pltpu.VMEM((n, 2, rows, kv_cols), bf16),
             pltpu.VMEM((rows, half), f32),
             pltpu.VMEM((up_chunks, experts, cap, up_rows), bf16),
             pltpu.VMEM((up_chunks, n, cap, up_rows), bf16),
@@ -447,8 +456,8 @@
             pltpu.VMEM((n, cap, LANES), bf16),
             pltpu.VMEM((arrivals, up_rows), bf16),
             pltpu.VMEM((arrivals, hidden_units), f32),
-            pltpu.VMEM((2, arrivals, part_units), bf16),
-            pltpu.VMEM((2, arrivals, part_units), bf16),
+            pltpu.VMEM((parts, arrivals, part_units), bf16),
+            pltpu.VMEM((parts, arrivals, part_units), bf16),
             pltpu.VMEM((arrivals, hidden_units), bf16),
             pltpu.VMEM((down_chunks, n, cap, down_cols), bf16),
             pltpu.VMEM((down_chunks, n, cap, down_cols), bf16),
@@ -458,18 +467,18 @@
             pltpu.VMEM((arrivals, LANES), f32),
             dma((up_chunks,)),
             dma((down_chunks,)),
-            dma((2, n)),
-            dma((2, n)),
-            dma((up_chunks, n)),
-            dma((up_chunks, n)),
-            dma((2,)),
-            dma((2,)),
-            dma((down_chunks, n)),
-            dma((down_chunks, n)),
+            dma((n,)),
+            dma((n,)),
+            dma((1,)),
+            dma((up_chunks,)),
+            dma((parts,)),
+            dma((parts,)),
+            dma((1,)),
+            dma((down_chunks,)),
             dma((3,)),
             dma((3,)),
-            dma((n,)),
-            dma((n,)),
+            dma((1,)),
+            dma((1,)),
             dma((11,)),
         ],
         compiler_params=pltpu.CompilerParams(

time: 35.7 us -> 33.5 us (0.938)
  Pallas kernels: 33.5 us -> 31.2 us
    pallas_call x1, Pallas kernels: 32.9 us -> 30.6 us  [fused(): pl.pallas_call(functools.partial(layer_kernel, n, experts, half * lax.axi...]
where the time goes in v2:
time: 33.5 us; the launch traced here: 33.2 us
  Pallas kernels  31.2 us (93%)
  between operations  1.93 us (6%)
    pallas_call x1, Pallas kernels, fused(): pl.pallas_call(functools.partial(layer_kernel, n, experts, half * lax.axi...  30.6 us

profile of v2, /device:TPU:1, one launch (start us, length us, event | category | flops | bytes accessed | tf_op | source)
XLA Modules:
  0.0 33.2 jit_solution(14523071198728273670)
XLA Ops:
  1.9 30.6 %layer.1 = (bf16[8,3072]{1,0:T(8,128)(2,1)S(1)}, f32[1,8]{1,0:T(1,128)S(1)}) custom-call(bf16[8,3072]{1,0:T(8,128)(2,1)} %refs_0_.1, bf16[8,3072]{1,0:T(8,128)(2,1)} %refs_1_.1, bf16[8,512]{1,0:T(8,128)(2,1)} %refs_2_.1, bf16[8,512]{1,0:T(8,128)(2,1)} %refs_3_.1, s32[2,8]{1,0:T(2,128)} %bitcast.10, s32[1]{0:T(128)S(6)} %copy.15.refs_5_, f32[1,3072]{1,0:T(1,128)} %bitcast.7, ...), custom_call_target="tpu_custom_call" | custom-call | tf_op jit(solution)/shard_map/layer/pallas_call | solution.py:434
  32.5 0.6 %store.1 = (bf16[8,3072]{1,0:T(8,128)(2,1)}, f32[1,8]{1,0:T(1,128)}) custom-call(bf16[8,3072]{1,0:T(8,128)(2,1)S(1)} %get-tuple-element.6.out_ref, f32[1,8]{1,0:T(1,128)S(1)} %get-tuple-element.7.val_ref), custom_call_target="tpu_custom_call" | custom-call | tf_op jit(solution)/shard_map/store/pallas_call | solution.py:503

commit v3 on v2

--- a/solution.py
+++ b/solution.py
@@ -45,8 +45,24 @@
     n,
     experts,
     width,
+    sem_shapes,
     *refs,
 ):
+    dma = pltpu.SemaphoreType.DMA
+    pl.run_scoped(
+        functools.partial(layer_body, n, experts, width, len(sem_shapes), *refs),
+        *[dma(shape) for shape in sem_shapes],
+    )
+
+
+def layer_body(
+    n,
+    experts,
+    width,
+    sem_count,
+    *refs,
+):
+    sems, refs = refs[len(refs) - sem_count :], refs[: len(refs) - sem_count]
     inputs, (out_ref, val_ref) = refs[:13], refs[13:15]
     places, scratch = refs[15:24], refs[24:]
     q_ref, stream_ref, routes_ref, len_ref = places[:4]
@@ -73,6 +89,8 @@
     small_in,
     sq_send,
     sq_in,
+    ) = scratch
+    (
     wup_sem,
     wdn_sem,
     kv_ss,
@@ -88,7 +106,7 @@
     t_ss,
     t_rs,
     in_sem,
-    ) = scratch
+    ) = sems
     group = lax.axis_index("groups")
     me = lax.axis_index("seq")
     core = lax.axis_index("tp")
@@ -292,14 +310,19 @@
     sq_send[...] = jnp.broadcast_to(ends[:, 0:1] + ends[:, 1:2], sq_send.shape)
     sq_copy = remote(sq_send, sq_in, s_ss.at[1], s_rs.at[1], partner)
     sq_copy.start()
+    def last_term(p):
+        cols = slice(p * part_units, (p + 1) * part_units)
+        return uown[:, cols] + jnp.dot(
+            xall[...], wup_v[up_chunks - 1, :, cols], preferred_element_type=jnp.float32
+        )
+
+    ready = last_term(0)
     for p in range(parts):
-        cols = slice(p * part_units, (p + 1) * part_units)
-        part = uown[:, cols] + jnp.dot(
-            xall[...], wup_v[up_chunks - 1, :, cols], preferred_element_type=jnp.float32
-        )
-        uown[:, cols] = part
-        usend[p] = part.astype(jnp.bfloat16)
+        after = last_term(p + 1) if p + 1 < parts else None
+        uown[:, p * part_units : (p + 1) * part_units] = ready
+        usend[p] = ready.astype(jnp.bfloat16)
         exchange(p).start()
+        ready = after
 
     sq_copy.wait_recv()
     scale = lax.rsqrt((sq_send[...] + sq_in[...])[:, 0:1] / width + eps)
@@ -431,8 +454,27 @@
     raw = pl.BlockSpec(memory_space=pl.ANY)
     bf16, f32 = jnp.bfloat16, jnp.float32
     dma = pltpu.SemaphoreType.DMA
+    sem_shapes = (
+        (up_chunks,),
+        (down_chunks,),
+        (n,),
+        (n,),
+        (1,),
+        (up_chunks,),
+        (parts,),
+        (parts,),
+        (1,),
+        (down_chunks,),
+        (3,),
+        (3,),
+        (1,),
+        (1,),
+        (11,),
+    )
     out, values = pl.pallas_call(
-        functools.partial(layer_kernel, n, experts, half * lax.axis_size("tp")),
+        functools.partial(
+            layer_kernel, n, experts, half * lax.axis_size("tp"), sem_shapes
+        ),
         out_shape=(pltpu.VMEM((rows, half), bf16), pltpu.VMEM((1, rows), f32)),
         in_specs=[hbm] * 13,
         out_specs=(vmem, vmem),
@@ -465,21 +507,6 @@
             pltpu.VMEM((2, rows, LANES), f32),
             pltpu.VMEM((arrivals, LANES), f32),
             pltpu.VMEM((arrivals, LANES), f32),
-            dma((up_chunks,)),
-            dma((down_chunks,)),
-            dma((n,)),
-            dma((n,)),
-            dma((1,)),
-            dma((up_chunks,)),
-            dma((parts,)),
-            dma((parts,)),
-            dma((1,)),
-            dma((down_chunks,)),
-            dma((3,)),
-            dma((3,)),
-            dma((1,)),
-            dma((1,)),
-            dma((11,)),
         ],
         compiler_params=pltpu.CompilerParams(
             collective_id=0, has_side_effects=True, vmem_limit_bytes=VMEM_BYTES

time: 33.5 us -> 32.6 us (0.973)
  Pallas kernels: 31.2 us -> 30.4 us
    pallas_call x1, Pallas kernels: 30.6 us -> 29.7 us  [fused(): pl.pallas_call(functools.partial(layer_kernel, n, experts, half * lax.axi...]
where the time goes in v3:
time: 32.6 us; the launch traced here: 32.3 us
  Pallas kernels  30.4 us (93%)
  between operations  1.93 us (6%)
    pallas_call x1, Pallas kernels, fused(): pl.pallas_call(functools.partial(layer_kernel, n, experts, half * lax.axi...  29.7 us

profile of v3, /device:TPU:1, one launch (start us, length us, event | category | flops | bytes accessed | tf_op | source)
XLA Modules:
  0.0 32.3 jit_solution(11783020350583294173)
XLA Ops:
  1.9 29.7 %layer.1 = (bf16[8,3072]{1,0:T(8,128)(2,1)S(1)}, f32[1,8]{1,0:T(1,128)S(1)}) custom-call(bf16[8,3072]{1,0:T(8,128)(2,1)} %refs_0_.1, bf16[8,3072]{1,0:T(8,128)(2,1)} %refs_1_.1, bf16[8,512]{1,0:T(8,128)(2,1)} %refs_2_.1, bf16[8,512]{1,0:T(8,128)(2,1)} %refs_3_.1, s32[2,8]{1,0:T(2,128)} %bitcast.10, s32[1]{0:T(128)S(6)} %copy.15.refs_5_, f32[1,3072]{1,0:T(1,128)} %bitcast.7, ...), custom_call_target="tpu_custom_call" | custom-call | tf_op jit(solution)/shard_map/layer/pallas_call | solution.py:474
  31.7 0.6 %store.1 = (bf16[8,3072]{1,0:T(8,128)(2,1)}, f32[1,8]{1,0:T(1,128)}) custom-call(bf16[8,3072]{1,0:T(8,128)(2,1)S(1)} %get-tuple-element.6.out_ref, f32[1,8]{1,0:T(1,128)S(1)} %get-tuple-element.7.val_ref), custom_call_target="tpu_custom_call" | custom-call | tf_op jit(solution)/shard_map/store/pallas_call | solution.py:530

commit v4 on v3

--- a/solution.py
+++ b/solution.py
@@ -10,7 +10,8 @@
 
 HD = 128
 LANES = 128
-SUB = 8
+TILE = 256
+ACCS = 16
 ROW_LIMIT = 64
 VMEM_BYTES = 66 * 1000 * 1000
 
@@ -45,13 +46,18 @@
     n,
     experts,
     width,
+    arrivals,
+    att_rows,
     sem_shapes,
     *refs,
 ):
     dma = pltpu.SemaphoreType.DMA
+    accumulators = [pltpu.ACC(spot % 2)((arrivals, TILE), jnp.float32) for spot in range(ACCS)]
+    accumulators += [pltpu.ACC(unit)((att_rows, TILE), jnp.float32) for unit in range(2)]
     pl.run_scoped(
         functools.partial(layer_body, n, experts, width, len(sem_shapes), *refs),
         *[dma(shape) for shape in sem_shapes],
+        *accumulators,
     )
 
 
@@ -62,6 +68,8 @@
     sem_count,
     *refs,
 ):
+    accs, att_accs = refs[len(refs) - ACCS - 2 : len(refs) - 2], refs[len(refs) - 2 :]
+    refs = refs[: len(refs) - ACCS - 2]
     sems, refs = refs[len(refs) - sem_count :], refs[: len(refs) - sem_count]
     inputs, (out_ref, val_ref) = refs[:13], refs[13:15]
     places, scratch = refs[15:24], refs[24:]
@@ -89,6 +97,8 @@
     small_in,
     sq_send,
     sq_in,
+    ktile,
+    vtile,
     ) = scratch
     (
     wup_sem,
@@ -133,8 +143,25 @@
     def other(step):
         return step + (step >= me).astype(jnp.int32)
 
+    turn = [0, 0]
+
+    def multiply(acc, unit, lhs, rhs, transpose=False):
+        register = turn[unit] % 2
+        turn[unit] += 1
+        pltpu.matmul_push_rhs(
+            rhs, staging_register=register, mxu_index=unit, transpose=transpose
+        )
+        pltpu.matmul_acc_lhs(acc, lhs, load_staged_rhs=register)
+
+    def accumulate(spot, lhs, rhs):
+        multiply(accs[spot], spot % 2, lhs, rhs)
+
     kvbuf[...] = jnp.zeros_like(kvbuf)
+    ktile[...] = jnp.zeros_like(ktile)
+    vtile[...] = jnp.zeros_like(vtile)
     barrier = pltpu.get_barrier_semaphore()
+    for acc in (*accs, *att_accs):
+        pltpu.matmul_pop(acc)
     for step in range(n - 1):
         pl.semaphore_signal(
             barrier, inc=1, device_id=(group, other(step), core), device_id_type=MESH
@@ -175,24 +202,24 @@
 
     route0 = upright(routes_ref[0:1, :])
     route1 = upright(routes_ref[1:2, :])
-    lower = (sooner < later).astype(jnp.float32).astype(jnp.bfloat16)
-
-    def slots(count, per_expert):
-        place = lax.broadcasted_iota(jnp.int32, (rows, count * cap), 1)
+    def slots(place, per_expert, count, line0, line1, axis):
         block = block_of(place, cap, count)
         expert = block_of(block, per_expert, experts)
         slot = (place - block * cap).astype(jnp.float32)
-        hits = ((route0 == expert) | (route1 == expert)).astype(jnp.float32)
-        rank = jnp.dot(lower, hits.astype(jnp.bfloat16), preferred_element_type=jnp.float32)
-        return expert, rank == slot
-
-    expert, at_slot = slots(experts, 1)
-    placing = (((route0 == expert) | (route1 == expert)) & at_slot).astype(jnp.float32)
-    placed = placing.astype(jnp.bfloat16)
-    expert_r, at_slot_r = slots(n, owners)
-    fetch0 = ((route0 == expert_r) & at_slot_r).astype(jnp.float32)
-    fetch1 = ((route1 == expert_r) & at_slot_r).astype(jnp.float32)
-    fetch = jnp.concatenate([fetch0, fetch1], axis=0).astype(jnp.bfloat16)
+        first, second = line0 == expert, line1 == expert
+        hits = (first | second).astype(jnp.float32)
+        token = lax.broadcasted_iota(jnp.int32, place.shape, axis)
+        rank = jnp.zeros(place.shape, jnp.float32)
+        for t in range(rows - 1):
+            own = hits[t : t + 1, :] if axis == 0 else hits[:, t : t + 1]
+            rank = rank + jnp.where(token > t, own, 0.0)
+        return first & (rank == slot), second & (rank == slot)
+
+    upper = lax.broadcasted_iota(jnp.int32, (experts * cap, rows), 0)
+    fill0, fill1 = slots(upper, 1, experts, routes_ref[0:1, :], routes_ref[1:2, :], 1)
+    filled = (fill0 | fill1).astype(jnp.float32)
+    across = lax.broadcasted_iota(jnp.int32, (rows, n * cap), 1)
+    back0, back1 = slots(across, owners, n, route0, route1, 0)
 
     for step in range(n - 1, 0, -1):
 
@@ -204,12 +231,10 @@
         down_copy(c).start()
 
     def pack(values):
-        return lax.dot_general(
-            placed,
-            values.astype(jnp.bfloat16),
-            (((0,), (0,)), ((), ())),
-            preferred_element_type=jnp.float32,
-        )
+        packed = jnp.zeros((experts * cap, values.shape[1]), jnp.float32)
+        for t in range(rows):
+            packed = packed + filled[:, t : t + 1] * values[t : t + 1, :]
+        return packed
 
     def dispatch(src_of, dst, send_sem, recv_sem):
         for step in range(n - 1):
@@ -217,39 +242,73 @@
             remote(src_of(to // owners), dst, send_sem, recv_sem, (group, to, core)).start()
 
     inv_root = 1.0 / math.sqrt(HD)
-    query_row = lax.broadcasted_iota(jnp.int32, (per_group, rows, keys), 1).reshape(
-        per_group * rows, keys
-    )
-    key_pos = lax.broadcasted_iota(jnp.int32, (per_group * rows, keys), 1)
+    att_rows = per_group * rows
+    query_row = lax.broadcasted_iota(jnp.int32, (per_group, rows, 2 * keys), 1).reshape(
+        att_rows, 2 * keys
+    )
+    spread = lax.broadcasted_iota(jnp.int32, (att_rows, 2 * keys), 1)
+    left = spread < keys
+    key_pos = jnp.where(left, spread, spread - keys)
     allowed = (key_pos <= me * rows + query_row) & (key_pos < len_ref[0])
+    pairs = kv_heads // 2
+
+    def block(which, head):
+        cols = slice(head * HD, (head + 1) * HD)
+        return kvbuf[:, which, :, cols].astype(jnp.float32).reshape(keys, HD).astype(jnp.bfloat16)
+
+    for pair in range(pairs):
+        for side in range(2):
+            down_rows = slice(side * keys, (side + 1) * keys)
+            cols = slice(side * HD, (side + 1) * HD)
+            ktile[pair, down_rows, cols] = block(0, 2 * pair + side)
+            vtile[pair, down_rows, cols] = block(1, 2 * pair + side)
     all_scores = []
-    for head in range(kv_heads):
-        cols = slice(head * HD, (head + 1) * HD)
-        k_head = kvbuf[:, 0, :, cols].astype(jnp.float32).reshape(keys, HD).astype(jnp.bfloat16)
-        base = head * per_group
-        q_head = jnp.concatenate(
-            [
-                q_ref[:, (base + g) * HD : (base + g + 1) * HD].astype(jnp.float32)
-                for g in range(per_group)
-            ],
-            axis=0,
-        ).astype(jnp.bfloat16)
-        all_scores.append(
-            lax.dot_general(
-                q_head, k_head, (((1,), (1,)), ((), ())), preferred_element_type=jnp.float32
+    for pair in range(pairs):
+        sides = []
+        for side in range(2):
+            base = (2 * pair + side) * per_group
+            sides.append(
+                jnp.concatenate(
+                    [
+                        q_ref[:, (base + g) * HD : (base + g + 1) * HD].astype(jnp.float32)
+                        for g in range(per_group)
+                    ],
+                    axis=0,
+                ).astype(jnp.bfloat16)
             )
-            * inv_root
+        unit = pair % 2
+        multiply(
+            att_accs[unit], unit, jnp.concatenate(sides, axis=1), ktile[pair], transpose=True
         )
+        if unit or pair == pairs - 1:
+            for done in range(pair - unit, pair + 1):
+                all_scores.append(pltpu.matmul_pop(att_accs[done % 2])[:, : 2 * keys] * inv_root)
+    all_weights, totals = [], []
+    for pair in range(pairs):
+        scores = jnp.where(allowed, all_scores[pair], masked)
+        tops = [
+            jnp.max(jnp.where(mine, scores, masked), axis=-1, keepdims=True)
+            for mine in (left, ~left)
+        ]
+        weights = jnp.where(allowed, jnp.exp(scores - jnp.where(left, tops[0], tops[1])), 0.0)
+        totals += [
+            jnp.sum(jnp.where(mine, weights, 0.0), axis=-1, keepdims=True)
+            for mine in (left, ~left)
+        ]
+        wide = [weights]
+        if 2 * keys < TILE:
+            wide.append(jnp.zeros((att_rows, TILE - 2 * keys), jnp.float32))
+        all_weights.append(jnp.concatenate(wide, axis=1).astype(jnp.bfloat16))
     updates = []
-    for head in range(kv_heads):
-        cols = slice(head * HD, (head + 1) * HD)
-        v_head = kvbuf[:, 1, :, cols].astype(jnp.float32).reshape(keys, HD).astype(jnp.bfloat16)
-        scores = jnp.where(allowed, all_scores[head], masked)
-        top = jnp.max(scores, axis=-1, keepdims=True)
-        weights = jnp.where(allowed, jnp.exp(scores - top), 0.0)
-        total = jnp.sum(weights, axis=-1, keepdims=True)
-        update = jnp.dot(weights.astype(jnp.bfloat16), v_head, preferred_element_type=jnp.float32)
-        updates.append(update / total)
+    for pair in range(pairs):
+        unit = pair % 2
+        multiply(att_accs[unit], unit, all_weights[pair], vtile[pair])
+        if unit or pair == pairs - 1:
+            for done in range(pair - unit, pair + 1):
+                both_sides = pltpu.matmul_pop(att_accs[done % 2])
+                for side in range(2):
+                    update = both_sides[:, side * HD : (side + 1) * HD]
+                    updates.append(update / totals[2 * done + side])
     squares = jnp.zeros((rows, 1), jnp.float32)
     chunks = []
     for c in range(up_chunks):
@@ -299,10 +358,17 @@
     def exchange(p):
         return remote(usend.at[p], uin.at[p], u_ss.at[p], u_rs.at[p], partner)
 
+    def up_tiles(c, spots):
+        for pair in range(spots.start, spots.stop, 2):
+            for k in range(up_rows // TILE):
+                deep = slice(k * TILE, (k + 1) * TILE)
+                for spot in (pair, pair + 1):
+                    cols = slice(spot * TILE, (spot + 1) * TILE)
+                    accumulate(spot, xall[:, deep], wup_v[c, deep, cols])
+
     for c in range(up_chunks - 1):
         xall[...] = gather_rows(c)
-        term = jnp.dot(xall[...], wup_v[c], preferred_element_type=jnp.float32)
-        uown[...] = term if c == 0 else uown[...] + term
+        up_tiles(c, range(ACCS))
 
     xall[...] = gather_rows(up_chunks - 1)
     arrival(xtail.at[others], t_rs.at[0]).wait_recv()
@@ -310,54 +376,95 @@
     sq_send[...] = jnp.broadcast_to(ends[:, 0:1] + ends[:, 1:2], sq_send.shape)
     sq_copy = remote(sq_send, sq_in, s_ss.at[1], s_rs.at[1], partner)
     sq_copy.start()
-    def last_term(p):
-        cols = slice(p * part_units, (p + 1) * part_units)
-        return uown[:, cols] + jnp.dot(
-            xall[...], wup_v[up_chunks - 1, :, cols], preferred_element_type=jnp.float32
-        )
-
-    ready = last_term(0)
+    per_part = ACCS // parts
+
+    def finish_part(p):
+        for spot in range(p * per_part, (p + 1) * per_part):
+            term = pltpu.matmul_pop(accs[spot])
+            uown[:, spot * TILE : (spot + 1) * TILE] = term
+            at = (spot - p * per_part) * TILE
+            usend[p, :, at : at + TILE] = term.astype(jnp.bfloat16)
+        exchange(p).start()
+
     for p in range(parts):
-        after = last_term(p + 1) if p + 1 < parts else None
-        uown[:, p * part_units : (p + 1) * part_units] = ready
-        usend[p] = ready.astype(jnp.bfloat16)
-        exchange(p).start()
-        ready = after
+        at = p * per_part
+        up_tiles(up_chunks - 1, range(at, at + 2))
+        if p:
+            finish_part(p - 1)
+        up_tiles(up_chunks - 1, range(at + 2, at + per_part))
+    finish_part(parts - 1)
 
     sq_copy.wait_recv()
     scale = lax.rsqrt((sq_send[...] + sq_in[...])[:, 0:1] / width + eps)
 
     def activate(p):
-        exchange(p).wait_recv()
         cols = slice(p * part_units, (p + 1) * part_units)
         up = (uown[:, cols] + uin[p].astype(jnp.float32)) * scale
         active[:, cols] = (up / (1.0 + jnp.exp(-up))).astype(jnp.bfloat16)
 
-    def send_back(c, down):
+    pieces_of = [(c, 0, down_cols) for c in range(down_chunks - 1)]
+    pieces_of += [(down_chunks - 1, lo, down_cols // 2) for lo in (0, down_cols // 2)]
+
+    def down_tiles(t, low, high):
+        c, lo, wide = pieces_of[t]
+        middle = units // TILE // 2
+        for k in range(low, high):
+            deep = slice(k * TILE, (k + 1) * TILE)
+            if wide == TILE:
+                spots = ((2 * t + k // middle, 0),)
+            else:
+                spots = tuple((2 * t + q, q) for q in range(wide // TILE))
+            for spot, q in spots:
+                cols = slice(lo + q * TILE, lo + (q + 1) * TILE)
+                accumulate(spot, active[:, deep], wdn_v[c, deep, cols])
+
+    def halves_tiles(t, low, high):
+        middle = units // TILE // 2
+        for k in range(low, high):
+            down_tiles(t, k, k + 1)
+            down_tiles(t, k + middle, k + middle + 1)
+
+    def send_back(t):
+        c, lo, wide = pieces_of[t]
+        cols = pl.ds(lo, wide)
+        terms = [pltpu.matmul_pop(accs[2 * t + q]) for q in range(2)]
+        down = terms[0] + terms[1] if wide == TILE else jnp.concatenate(terms, axis=1)
         for d in range(n):
-            rsend[c, d] = down[d * cap : (d + 1) * cap].astype(jnp.bfloat16)
+            rsend[c, d, :, cols] = down[d * cap : (d + 1) * cap].astype(jnp.bfloat16)
         for step in range(n - 1):
             to = other(step)
             remote(
-                rsend.at[c, to], rin.at[c, me], r_ss.at[0], r_rs.at[c], (group, to, core)
+                rsend.at[c, to, :, cols],
+                rin.at[c, me, :, cols],
+                r_ss.at[0],
+                r_rs.at[t],
+                (group, to, core),
             ).start()
-        rin[c, me] = rsend[c, me]
-
-    first = min(2, down_chunks)
-    downs = [None] * first
+        rin[c, me, :, cols] = rsend[c, me, :, cols]
+
+    for c in range(down_chunks):
+        down_copy(c).wait()
+    per_part = part_units // TILE
+    for p in range(parts - 1):
+        exchange(p).wait_recv()
     for p in range(parts):
+        if p == parts - 1:
+            exchange(p).wait_recv()
         activate(p)
-        span = slice(p * part_units, (p + 1) * part_units)
-        for c in range(first):
-            if p == 0:
-                down_copy(c).wait()
-            term = jnp.dot(active[:, span], wdn_v[c, span], preferred_element_type=jnp.float32)
-            downs[c] = term if p == 0 else downs[c] + term
-    for c in range(first):
-        send_back(c, downs[c])
-    for c in range(first, down_chunks):
-        down_copy(c).wait()
-        send_back(c, jnp.dot(active[...], wdn_v[c], preferred_element_type=jnp.float32))
+        for t in range(2):
+            down_tiles(t, p * per_part, (p + 1) * per_part)
+    send_back(0)
+    depth = units // TILE
+    for t in range(2, len(pieces_of)):
+        if pieces_of[t][2] == TILE:
+            halves_tiles(t, 0, 2)
+            send_back(t - 1)
+            halves_tiles(t, 2, depth // 2)
+        else:
+            down_tiles(t, 0, 4)
+            send_back(t - 1)
+            down_tiles(t, 4, depth)
+    send_back(len(pieces_of) - 1)
 
     stat_copy.wait_recv()
     both = small_send[0] + small_in[0]
@@ -368,14 +475,20 @@
     gate0 = 1.0 / (1.0 + jnp.exp(picked1 - picked0))
     gate1 = 1.0 / (1.0 + jnp.exp(picked0 - picked1))
 
+    coeff = gate0 * back0.astype(jnp.float32) + gate1 * back1.astype(jnp.float32)
     sq_part = jnp.zeros((rows, 1), jnp.float32)
     dot_part = jnp.zeros((rows, 1), jnp.float32)
-    for c in range(down_chunks):
-        arrival(rin.at[c, others], r_rs.at[c]).wait_recv()
-        pieces = jnp.concatenate([rin[c, d].astype(jnp.float32) for d in range(n)], axis=0)
-        fetched = jnp.dot(fetch, pieces.astype(jnp.bfloat16), preferred_element_type=jnp.float32)
-        cols = slice(c * down_cols, (c + 1) * down_cols)
-        final = hid[:, cols] + (gate0 * fetched[:rows] + gate1 * fetched[rows:])
+    for t, (c, lo, wide) in enumerate(pieces_of):
+        span = slice(lo, lo + wide)
+        arrival(rin.at[c, others, :, span], r_rs.at[t]).wait_recv()
+        cols = slice(c * down_cols + lo, c * down_cols + lo + wide)
+        sums = [hid[:, cols], jnp.zeros((rows, wide), jnp.float32)]
+        for d in range(n):
+            piece = rin[c, d, :, span].astype(jnp.float32)
+            for slot in range(cap):
+                spot = d * cap + slot
+                sums[slot % 2] += coeff[:, spot : spot + 1] * piece[slot : slot + 1, :]
+        final = sums[0] + sums[1]
         out_ref[:, cols] = final.astype(jnp.bfloat16)
         sq_part = sq_part + jnp.sum(final * final, axis=1, keepdims=True)
         dot_part = dot_part + jnp.sum(
@@ -448,6 +561,7 @@
     down_cols = largest(half, 512)
     down_chunks = half // down_cols
     parts = 4
+    att_rows = up_rows // HD * rows
     part_units = hidden_units // parts
     vmem = pl.BlockSpec(memory_space=pltpu.VMEM)
     hbm = pl.BlockSpec(memory_space=pltpu.HBM)
@@ -464,7 +578,7 @@
         (parts,),
         (parts,),
         (1,),
-        (down_chunks,),
+        (down_chunks + 1,),
         (3,),
         (3,),
         (1,),
@@ -473,7 +587,7 @@
     )
     out, values = pl.pallas_call(
         functools.partial(
-            layer_kernel, n, experts, half * lax.axis_size("tp"), sem_shapes
+            layer_kernel, n, experts, half * lax.axis_size("tp"), arrivals, att_rows, sem_shapes
         ),
         out_shape=(pltpu.VMEM((rows, half), bf16), pltpu.VMEM((1, rows), f32)),
         in_specs=[hbm] * 13,
@@ -507,6 +621,8 @@
             pltpu.VMEM((2, rows, LANES), f32),
             pltpu.VMEM((arrivals, LANES), f32),
             pltpu.VMEM((arrivals, LANES), f32),
+            pltpu.VMEM((up_chunks // 2, TILE, TILE), bf16),
+            pltpu.VMEM((up_chunks // 2, TILE, TILE), bf16),
         ],
         compiler_params=pltpu.CompilerParams(
             collective_id=0, has_side_effects=True, vmem_limit_bytes=VMEM_BYTES
@@ -653,7 +769,15 @@
     stream, w_up = args[0], args[8]
     arrivals = lax.axis_size("seq") * (stream.shape[0] // 2)
     weight_bytes = 4 * w_up.shape[0] * w_up.shape[1]
-    small = arrivals <= ROW_LIMIT and weight_bytes <= 52 * 1024 * 1024
+    kv_heads = args[2].shape[1] // HD
+    keys = lax.axis_size("seq") * stream.shape[0]
+    tiled = (
+        w_up.shape[1] == ACCS * TILE
+        and stream.shape[1] % (kv_heads * TILE) == 0
+        and kv_heads % 2 == 0
+        and 2 * keys <= TILE
+    )
+    small = tiled and arrivals <= ROW_LIMIT and weight_bytes <= 52 * 1024 * 1024
     return fused(*args) if small else unfused(*args)
 
 

time: 32.6 us -> 32.6 us (level)
  no operation moved by 1% of the time
where the time goes in v4:
time: 32.6 us; the launch traced here: 32.3 us
  Pallas kernels  30.4 us (93%)
  between operations  1.93 us (6%)
    pallas_call x1, Pallas kernels, fused(): pl.pallas_call(functools.partial(layer_kernel, n, experts, half * lax.axi...  29.8 us

profile of v4, /device:TPU:1, one launch (start us, length us, event | category | flops | bytes accessed | tf_op | source)
XLA Modules:
  0.0 32.3 jit_solution(7056032786049872619)
XLA Ops:
  1.9 29.8 %layer.1 = (bf16[8,3072]{1,0:T(8,128)(2,1)S(1)}, f32[1,8]{1,0:T(1,128)S(1)}) custom-call(bf16[8,3072]{1,0:T(8,128)(2,1)} %refs_0_.1, bf16[8,3072]{1,0:T(8,128)(2,1)} %refs_1_.1, bf16[8,512]{1,0:T(8,128)(2,1)} %refs_2_.1, bf16[8,512]{1,0:T(8,128)(2,1)} %refs_3_.1, s32[2,8]{1,0:T(2,128)} %bitcast.10, s32[1]{0:T(128)S(6)} %copy.15.refs_5_, f32[1,3072]{1,0:T(1,128)} %bitcast.7, ...), custom_call_target="tpu_custom_call" | custom-call | tf_op jit(solution)/shard_map/layer/pallas_call | solution.py:588
  31.7 0.6 %store.1 = (bf16[8,3072]{1,0:T(8,128)(2,1)}, f32[1,8]{1,0:T(1,128)}) custom-call(bf16[8,3072]{1,0:T(8,128)(2,1)S(1)} %get-tuple-element.6.out_ref, f32[1,8]{1,0:T(1,128)S(1)} %get-tuple-element.7.val_ref), custom_call_target="tpu_custom_call" | custom-call | tf_op jit(solution)/shard_map/store/pallas_call | solution.py:646
